TPU v7x, 32 devices: a whole 2x2x4 slice. The times are simulated.
32 devices in a mesh: dp: 8 (over z, x), head: 4 (over y, core).
Axes of the slice: x: 2, y: 2, z: 4, core: 2. Of those that a mesh axis runs over, the one named last changes fastest.
Arguments:
- inputs: bfloat16 [8192, 2048], P('dp'), may hold values from -6 to 6
- lengths: int32 [8], P('dp'), may hold values from 256 to 1024, as said below
- gain_attn: bfloat16 [2048], P('dp'), may hold values from 0.5 to 1.5
- w_query: bfloat16 [2048, 2048], P('dp', 'head'), may hold values from -0.25 to 0.25
- w_key: bfloat16 [2048, 2048], P('dp', 'head'), may hold values from -0.25 to 0.25
- w_value: bfloat16 [2048, 2048], P('dp', 'head'), may hold values from -0.125 to 0.125
- w_slot: bfloat16 [2048, 256], P('dp', 'head'), may hold values from -0.125 to 0.125
- gate_bias: float32 [256], P('head'), may hold values from 0 to 8
- w_out: bfloat16 [2048, 2048], P('head', 'dp'), may hold values from -0.5 to 0.5
- gain_ffn: bfloat16 [2048], P('dp'), may hold values from 0.5 to 1.5
- w_gate: bfloat16 [2048, 5632], P('dp', 'head'), may hold values from -0.125 to 0.125
- w_up: bfloat16 [2048, 5632], P('dp', 'head'), may hold values from -0.125 to 0.125
- w_down: bfloat16 [5632, 2048], P('head', 'dp'), may hold values from -0.078125 to 0.078125
- cotangent: bfloat16 [8192, 2048], P('dp'), may hold values from -6 to 6
Outputs:
- output: bfloat16 [8192, 2048], P('dp')
- grad_inputs: float32 [8192, 2048], P('dp')
- grad_gain_attn: float32 [2048], P('dp')
- grad_w_query: float32 [2048, 2048], P('dp', 'head')
- grad_w_key: float32 [2048, 2048], P('dp', 'head')
- grad_w_value: float32 [2048, 2048], P('dp', 'head')
- grad_w_slot: float32 [2048, 256], P('dp', 'head')
- grad_gate_bias: float32 [256], P('head')
- grad_w_out: float32 [2048, 2048], P('head', 'dp')
- grad_gain_ffn: float32 [2048], P('dp')
- grad_w_gate: float32 [2048, 5632], P('dp', 'head')
- grad_w_up: float32 [2048, 5632], P('dp', 'head')
- grad_w_down: float32 [5632, 2048], P('head', 'dp')
Inputs may be any that keep to these rules, and one draw needn't show every extreme that they name: lengths[s] is the number of valid leading positions of sequence s; some sequence has all 1024 valid.
All inputs are finite; a program needn't handle non-finite values.
Results may differ from a plain program's by a relative error of at most 0.014.
Values may be sent and summed in bfloat16 or wider, within the bound.
A program may use at most 256 MiB of HBM per device.

v0:
```python
import jax
import jax.numpy as jnp
from jax import lax
from jax.sharding import PartitionSpec as P

SPAN = 64


epsilon = 1e-06
damping = 8.0
highest = lax.Precision.HIGHEST


def norm_rows(values, gain):
    factor = lax.rsqrt(jnp.mean(values * values, axis=-1, keepdims=True) + epsilon)
    return values * factor * gain


def swiglu(gate_act, up_act):
    return jax.nn.silu(gate_act) * up_act


def span_step(states, pieces):
    queries, key_rows, value_rows, logdecay, writes = pieces
    state_keys, state_values = states
    rows_count = queries.shape[0]
    cumul = jnp.cumsum(logdecay, axis=0)
    causal = (jnp.arange(rows_count)[:, None] >= jnp.arange(rows_count)[None, :])[:, :, None]
    spread = jnp.where(causal, cumul[:, None, :] - cumul[None, :, :], 0.0)
    weighted = jnp.where(causal, jnp.exp(spread), 0.0) * writes[None, :, :]
    scale_factor = queries.shape[1] ** (-0.5)
    inner_products = jnp.dot(queries, key_rows.T, precision=highest) * scale_factor
    carried = jnp.dot(queries, state_keys.T, precision=highest) * scale_factor
    scores = jnp.exp(cumul) * carried + jnp.einsum(
        "tsj,ts->tj", weighted, inner_products, precision=highest
    )
    slot_probs = jax.nn.softmax(scores, axis=-1)
    mixing = jnp.einsum("tj,tsj->ts", slot_probs, weighted, precision=highest)
    result = jnp.dot(slot_probs * jnp.exp(cumul), state_values, precision=highest) + jnp.dot(
        mixing, value_rows, precision=highest
    )
    last_cumul = cumul[-1]
    tail_weight = jnp.exp(last_cumul[None, :] - cumul) * writes
    new_keys = jnp.exp(last_cumul)[:, None] * state_keys + jnp.dot(
        tail_weight.T, key_rows, precision=highest
    )
    new_values = jnp.exp(last_cumul)[:, None] * state_values + jnp.dot(
        tail_weight.T, value_rows, precision=highest
    )
    return ((new_keys, new_values), result)


def slot_mixer(queries, key_rows, value_rows, gate_logits, valid_mask):
    logdecay = valid_mask[:, None] * jax.nn.log_sigmoid(gate_logits) / damping
    writes = valid_mask[:, None] * (1.0 - jnp.exp(logdecay))
    length = queries.shape[0]
    blocks = length // SPAN

    def blocked(matrix):
        return matrix.reshape(blocks, SPAN, matrix.shape[1])

    start_state = (
        jnp.zeros((gate_logits.shape[1], key_rows.shape[1]), jnp.float32),
        jnp.zeros((gate_logits.shape[1], value_rows.shape[1]), jnp.float32),
    )
    _, outputs = lax.scan(
        jax.checkpoint(span_step),
        start_state,
        (
            blocked(queries),
            blocked(key_rows),
            blocked(value_rows),
            blocked(logdecay),
            blocked(writes),
        ),
    )
    return outputs.reshape(length, value_rows.shape[1]) * valid_mask[:, None]


def matmul_low(left, right):
    return jnp.dot(left, right, preferred_element_type=jnp.float32)


def per_device(
    inputs,
    lengths,
    gain_attn,
    w_query,
    w_key,
    w_value,
    w_slot,
    gate_bias,
    w_out,
    gain_ffn,
    w_gate,
    w_up,
    w_down,
    cotangent,
):
    column_set = (
        lax.all_gather(gain_attn, "dp", axis=0, tiled=True),
        lax.all_gather(gain_ffn, "dp", axis=0, tiled=True),
        lax.all_gather(w_query, "dp", axis=0, tiled=True),
        lax.all_gather(w_key, "dp", axis=0, tiled=True),
        lax.all_gather(w_value, "dp", axis=0, tiled=True),
        lax.all_gather(w_slot, "dp", axis=0, tiled=True),
        lax.all_gather(w_gate, "dp", axis=0, tiled=True),
        lax.all_gather(w_up, "dp", axis=0, tiled=True),
    )
    row_set = (
        lax.all_gather(w_out, "dp", axis=1, tiled=True),
        lax.all_gather(w_down, "dp", axis=1, tiled=True),
    )
    (
        full_gain_attn,
        full_gain_ffn,
        full_query,
        full_key,
        full_value,
        full_slot,
        full_gate,
        full_up,
    ) = column_set
    full_out, full_down = row_set
    rows_in = inputs.astype(jnp.float32)
    length = rows_in.shape[0]
    valid_mask = (jnp.arange(length) < lengths[0]).astype(jnp.float32)
    normed, norm_attn_pull = jax.vjp(norm_rows, rows_in, full_gain_attn.astype(jnp.float32))
    normed_low = normed.astype(jnp.bfloat16)
    queries = matmul_low(normed_low, full_query).astype(jnp.bfloat16)
    key_proj = matmul_low(normed_low, full_key).astype(jnp.bfloat16)
    value_proj = matmul_low(normed_low, full_value).astype(jnp.bfloat16)
    gate_logits = matmul_low(normed_low, full_slot) + gate_bias

    def mixer_local(query_in, key_in, value_in, logit_in):
        return slot_mixer(query_in, key_in, value_in, logit_in, valid_mask)

    mixed, mixer_pull = jax.vjp(
        mixer_local,
        queries.astype(jnp.float32),
        key_proj.astype(jnp.float32),
        value_proj.astype(jnp.float32),
        gate_logits,
    )
    mixed_low = mixed.astype(jnp.bfloat16)
    resid = rows_in + lax.psum(matmul_low(mixed_low, full_out), "head")
    normed2, norm_ffn_pull = jax.vjp(norm_rows, resid, full_gain_ffn.astype(jnp.float32))
    normed2_low = normed2.astype(jnp.bfloat16)
    gate_act = matmul_low(normed2_low, full_gate)
    up_act = matmul_low(normed2_low, full_up)
    hidden, swiglu_pull = jax.vjp(swiglu, gate_act, up_act)
    hidden_low = hidden.astype(jnp.bfloat16)
    output_low = (
        resid
        + lax.psum(matmul_low(hidden_low, full_down).astype(jnp.bfloat16), "head").astype(
            jnp.float32
        )
    ).astype(jnp.bfloat16)
    back_cols = (
        lax.all_gather(w_query, "dp", axis=0, tiled=True),
        lax.all_gather(w_key, "dp", axis=0, tiled=True),
        lax.all_gather(w_value, "dp", axis=0, tiled=True),
        lax.all_gather(w_slot, "dp", axis=0, tiled=True),
        lax.all_gather(w_gate, "dp", axis=0, tiled=True),
        lax.all_gather(w_up, "dp", axis=0, tiled=True),
    )
    back_rows = (
        lax.all_gather(w_out, "dp", axis=1, tiled=True),
        lax.all_gather(w_down, "dp", axis=1, tiled=True),
    )
    full_query, full_key, full_value, full_slot, full_gate, full_up = back_cols
    full_out, full_down = back_rows
    d_hidden = matmul_low(cotangent, full_down.T)
    d_gate, d_up = swiglu_pull(d_hidden)
    d_gate_low = d_gate.astype(jnp.bfloat16)
    d_up_low = d_up.astype(jnp.bfloat16)
    grad_down = matmul_low(hidden_low.T, cotangent)
    grad_gate = matmul_low(normed2_low.T, d_gate_low)
    grad_up = matmul_low(normed2_low.T, d_up_low)
    d_normed2 = lax.psum(
        matmul_low(d_gate_low, full_gate.T) + matmul_low(d_up_low, full_up.T), "head"
    )
    d_resid_norm, grad_gain_ffn = norm_ffn_pull(d_normed2)
    d_resid = cotangent.astype(jnp.float32) + d_resid_norm
    d_attn_low = d_resid.astype(jnp.bfloat16)
    grad_out = matmul_low(mixed_low.T, d_attn_low)
    d_mixed = matmul_low(d_attn_low, full_out.T)
    d_query, d_key, d_value, d_logit = mixer_pull(d_mixed)
    grad_bias_part = jnp.sum(d_logit, axis=0)
    d_query_low = d_query.astype(jnp.bfloat16)
    d_key_low = d_key.astype(jnp.bfloat16)
    d_value_low = d_value.astype(jnp.bfloat16)
    d_logit_low = d_logit.astype(jnp.bfloat16)
    grad_query = matmul_low(normed_low.T, d_query_low)
    grad_key = matmul_low(normed_low.T, d_key_low)
    grad_value = matmul_low(normed_low.T, d_value_low)
    grad_slot = matmul_low(normed_low.T, d_logit_low)
    d_normed_part = (
        matmul_low(d_query_low, full_query.T)
        + matmul_low(d_key_low, full_key.T)
        + matmul_low(d_value_low, full_value.T)
        + matmul_low(d_logit_low, full_slot.T)
    )
    d_normed = lax.psum(d_normed_part.astype(jnp.bfloat16), "head").astype(jnp.float32)
    d_inputs_norm, grad_gain_attn = norm_attn_pull(d_normed)
    grad_inputs = d_resid + d_inputs_norm
    column_grads = (
        lax.psum_scatter(grad_gain_attn, "dp", scatter_dimension=0, tiled=True),
        lax.psum_scatter(grad_gain_ffn, "dp", scatter_dimension=0, tiled=True),
        lax.psum_scatter(grad_query, "dp", scatter_dimension=0, tiled=True),
        lax.psum_scatter(grad_key, "dp", scatter_dimension=0, tiled=True),
        lax.psum_scatter(grad_value, "dp", scatter_dimension=0, tiled=True),
        lax.psum_scatter(grad_slot, "dp", scatter_dimension=0, tiled=True),
        lax.psum_scatter(grad_gate, "dp", scatter_dimension=0, tiled=True),
        lax.psum_scatter(grad_up, "dp", scatter_dimension=0, tiled=True),
    )
    row_grads = (
        lax.psum_scatter(
            grad_out.astype(jnp.bfloat16), "dp", scatter_dimension=1, tiled=True
        ).astype(jnp.float32),
        lax.psum_scatter(
            grad_down.astype(jnp.bfloat16), "dp", scatter_dimension=1, tiled=True
        ).astype(jnp.float32),
    )
    grad_bias = lax.psum(grad_bias_part, "dp")
    return (
        output_low,
        grad_inputs,
        column_grads[0],
        column_grads[2],
        column_grads[3],
        column_grads[4],
        column_grads[5],
        grad_bias,
        row_grads[0],
        column_grads[1],
        column_grads[6],
        column_grads[7],
        row_grads[1],
    )


def solution(mesh):
    in_specs = (
        P("dp", None),
        P("dp"),
        P("dp"),
        P("dp", "head"),
        P("dp", "head"),
        P("dp", "head"),
        P("dp", "head"),
        P("head"),
        P("head", "dp"),
        P("dp"),
        P("dp", "head"),
        P("dp", "head"),
        P("head", "dp"),
        P("dp", None),
    )
    out_specs = (
        P("dp", None),
        P("dp", None),
        P("dp"),
        P("dp", "head"),
        P("dp", "head"),
        P("dp", "head"),
        P("dp", "head"),
        P("head"),
        P("head", "dp"),
        P("dp"),
        P("dp", "head"),
        P("dp", "head"),
        P("head", "dp"),
    )
    return jax.shard_map(
        per_device, mesh=mesh, in_specs=in_specs, out_specs=out_specs, check_vma=False
    )
```

profile of v0, /device:TPU:0, one launch (start us, length us, event | category | flops | bytes accessed | tf_op | source)
XLA Modules:
  0.0 2579.3 jit_solution(14699896438426582661)
XLA Ops:
  13.9 22.4 all-gather
  37.0 31.8 %all_gather.39 = bf16[2048,64]{0,1:T(8,128)(2,1)S(1)} all-gather(bf16[256,64]{0,1:T(8,128)(2,1)S(1)} %copy-done.20), channel_id=1, replica_groups=mesh['dp'=8,'head'=4] {'dp'}, dimensions={0}, use_global_device_ids=true | all-gather | bytes 294912 | tf_op jit(solution)/shard_map/all_gather | solution.py:106
  80.9 34.3 %all-gather.10.cloned.1.call-done = bf16[2048,512]{1,0:T(8,128)(2,1)} async-done(((bf16[256,512]{1,0:T(8,128)(2,1)}), bf16[2048,512]{1,0:T(8,128)(2,1)}) %all-gather.10.cloned.1.call-update) | async-done | bytes 2097168 | tf_op jit(solution)/shard_map/all_gather | solution.py:104
  122.0 43.0 %all-gather.12.cloned.1.call-done = bf16[2048,512]{1,0:T(8,128)(2,1)} async-done(((bf16[256,512]{1,0:T(8,128)(2,1)}), bf16[2048,512]{1,0:T(8,128)(2,1)}) %all-gather.12.cloned.1.call-update) | async-done | bytes 2097168 | tf_op jit(solution)/shard_map/all_gather | solution.py:105
  175.0 216.4 %while.52 = (s32[]{:T(128)}, f32[64,512]{1,0:T(8,128)S(1)}, f32[64,512]{1,0:T(8,128)S(1)}, f32[16,64,512]{2,1,0:T(8,128)}, f32[16,64,512]{2,1,0:T(8,128)}, /*ind...) while((s32[]{:T(128)}, f32[64,512]{1,0:T(8,128)S(1)}, ...), condition=%wide.region_5.6_spmd.clone.clone.clone, body=%wide.region_1.5_spmd.clone.clone.sunk.clone | while | flops 157441920 | bytes 3196303 | solution.py:66
  404.8 18.2 all-gather.1
  422.9 131.2 %all-reduce.9.cloned.1.call-done = f32[1024,2048]{1,0:T(8,128)} async-done(((f32[1024,2048]{1,0:T(8,128)}), f32[1024,2048]{1,0:T(8,128)}) %all-reduce.9.cloned.1.call-update) | async-done | bytes 8388624 | tf_op jit(solution)/shard_map/psum | solution.py:146
  566.0 82.7 %all-gather.18.cloned.1.call-done = bf16[2048,1408]{1,0:T(8,128)(2,1)} async-done(((bf16[256,1408]{1,0:T(8,128)(2,1)}), bf16[2048,1408]{1,0:T(8,128)(2,1)}) %all-gather.18.cloned.1.call-update) | async-done | bytes 5767184 | tf_op jit(solution)/shard_map/all_gather | solution.py:107
  648.7 11.9 fusion.151
  660.7 80.8 %all-gather.20.cloned.1.call-done = bf16[2048,1408]{1,0:T(8,128)(2,1)} async-done(((bf16[256,1408]{1,0:T(8,128)(2,1)}), bf16[2048,1408]{1,0:T(8,128)(2,1)}) %all-gather.20.cloned.1.call-update) | async-done | bytes 5767184 | tf_op jit(solution)/shard_map/all_gather | solution.py:108
  741.4 11.7 fusion.152
  753.1 81.7 %all-gather.22.cloned.1.call-done = bf16[1408,2048]{1,0:T(8,128)(2,1)} async-done(((bf16[1408,256]{1,0:T(8,128)(2,1)}), bf16[1408,2048]{1,0:T(8,128)(2,1)}) %all-gather.22.cloned.1.call-update) | async-done | bytes 5767184 | tf_op jit(solution)/shard_map/all_gather | solution.py:112
  834.8 15.6 multiply_convert_fusion.1
  850.4 10.9 fusion.153
  872.4 12.1 convolution_convert_fusion.1
  884.5 137.0 %all-reduce.11.cloned.1.call-done = f32[1024,2048]{1,0:T(8,128)} async-done(((f32[1024,2048]{1,0:T(8,128)}), f32[1024,2048]{1,0:T(8,128)}) %all-reduce.11.cloned.1.call-update) | async-done | bytes 8388624 | tf_op jit(solution)/shard_map/psum | solution.py:180
  1041.4 429.3 %while.51 = (s32[]{:T(128)}, f32[64,512]{1,0:T(8,128)S(1)}, f32[64,512]{1,0:T(8,128)S(1)}, bf16[16,64,512]{2,1,0:T(8,128)(2,1)S(1)}, bf16[16,64,512]{2,1,0:T(8,1...) while((s32[]{:T(128)}, f32[64,512]{1,0:T(8,128)S(1)}, ...), condition=%wide.region_23.24_spmd.clone.clone, body=%wide.region_11.0_spmd.clone.sunk.clone | while | flops 373932032 | bytes 8373975 | solution.py:66
  1489.0 9.5 add_convert_fusion
  1506.8 10.9 convolution_convert_fusion
  1542.7 12.2 fusion.160
  1555.0 12.0 fusion.161
  1568.9 82.8 %all-reduce.13.cloned.1.call-done = (bf16[1024,2048]{1,0:T(8,128)(2,1)}, bf16[1024,2048]{1,0:T(8,128)(2,1)}) async-done(((bf16[1024,2048]{1,0:T(8,128)(2,1)}, bf16[1024,2048]{1,0:T(8,128)(2,1)}), (bf16[1024,2048]{1,0:T(8,128)(2,1)}, bf16[1024,2048]{1,0:T(8,128)(2,1)})) %all-reduce.13.cloned.1.call-update) | async-done | bytes 8388624 | tf_op jit(solution)/shard_map/psum | solution.py:155
  1657.6 38.2 %all-reduce.3 = (f32[2048]{0:T(1024)S(1)}, f32[64]{0:T(128)}, f32[2048]{0:T(1024)S(1)}) all-reduce(f32[2048]{0:T(1024)S(1)} %get-tuple-element.768, f32[64]{0:T(128)S(1)} %neg.61, f32[2048]{0:T(1024)S(1)} %get-tuple-element.766), channel_id=2, replica_groups=mesh['dp'=8,'head'=4] {'dp'}, use_global_device_ids=true, to_apply=%region_27.28.clone | all-reduce | flops 4160 | bytes 33280
  1697.0 27.3 %reduce-scatter.17.cloned.1.call-done = bf16[512,256]{1,0:T(8,128)(2,1)} async-done(((bf16[512,2048]{1,0:T(8,128)(2,1)}), bf16[512,256]{1,0:T(8,128)(2,1)}) %reduce-scatter.17.cloned.1.call-update) | async-done | bytes 262160 | tf_op jit(solution)/shard_map/reduce_scatter | solution.py:218
  1726.1 17.2 fusion.119
  1743.3 94.6 %reduce-scatter.23.cloned.1.call-done = bf16[1408,256]{1,0:T(8,128)(2,1)} async-done(((bf16[1408,2048]{1,0:T(8,128)(2,1)}), bf16[1408,256]{1,0:T(8,128)(2,1)}) %reduce-scatter.23.cloned.1.call-update) | async-done | bytes 720912 | tf_op jit(solution)/shard_map/reduce_scatter | solution.py:221
  1840.2 64.1 %reduce-scatter.15.cloned.1.call-done = f32[256,64]{0,1:T(8,128)} async-done(((f32[2048,64]{0,1:T(8,128)}), f32[256,64]{0,1:T(8,128)}) %reduce-scatter.15.cloned.1.call-update) | async-done | bytes 65552 | tf_op jit(solution)/shard_map/reduce_scatter | solution.py:213
  1904.2 91.4 %reduce-scatter.11.cloned.1.call-done = f32[256,512]{1,0:T(8,128)} async-done(((f32[2048,512]{1,0:T(8,128)}), f32[256,512]{1,0:T(8,128)}) %reduce-scatter.11.cloned.1.call-update) | async-done | bytes 524304 | tf_op jit(solution)/shard_map/reduce_scatter | solution.py:211
  1995.7 92.0 %reduce-scatter.13.cloned.1.call-done = f32[256,512]{1,0:T(8,128)} async-done(((f32[2048,512]{1,0:T(8,128)}), f32[256,512]{1,0:T(8,128)}) %reduce-scatter.13.cloned.1.call-update) | async-done | bytes 524304 | tf_op jit(solution)/shard_map/reduce_scatter | solution.py:212
  2087.7 92.0 %reduce-scatter.9.cloned.1.call-done = f32[256,512]{1,0:T(8,128)} async-done(((f32[2048,512]{1,0:T(8,128)}), f32[256,512]{1,0:T(8,128)}) %reduce-scatter.9.cloned.1.call-update) | async-done | bytes 524304 | tf_op jit(solution)/shard_map/reduce_scatter | solution.py:210
  2179.8 196.5 %reduce-scatter.19.cloned.1.call-done = f32[256,1408]{1,0:T(8,128)} async-done(((f32[2048,1408]{1,0:T(8,128)}), f32[256,1408]{1,0:T(8,128)}) %reduce-scatter.19.cloned.1.call-update) | async-done | bytes 1441808 | tf_op jit(solution)/shard_map/reduce_scatter | solution.py:214
  2376.3 196.0 %reduce-scatter.21.cloned.1.call-done = f32[256,1408]{1,0:T(8,128)} async-done(((f32[2048,1408]{1,0:T(8,128)}), f32[256,1408]{1,0:T(8,128)}) %reduce-scatter.21.cloned.1.call-update) | async-done | bytes 1441808 | tf_op jit(solution)/shard_map/reduce_scatter | solution.py:215
  (1088 shorter events, 796.5 us)
Async XLA Ops:
  7.2 29.8 %copy-start.20 = (bf16[256,64]{0,1:T(8,128)(2,1)S(1)}, bf16[256,64]{0,1:T(8,128)(2,1)}, u32[]{:S(2)}) copy-start(bf16[256,64]{0,1:T(8,128)(2,1)} %param.24) | copy-start | bytes 98308
  7.2 68.2 %all-gather.14.cloned.1.call-start = ((), (), s32[]{:S(2)}) async-start(), calls=%async_computation.10 | async-start | bytes 2359296 | tf_op jit(solution)/shard_map/all_gather | solution.py:103
  7.9 107.3 %all-gather.10.cloned.1.call-start = ((), (), s32[]{:S(2)}) async-start(), calls=%async_computation.8 | async-start | bytes 2359296 | tf_op jit(solution)/shard_map/all_gather | solution.py:104
  8.7 156.3 %all-gather.12.cloned.1.call-start = ((), (), s32[]{:S(2)}) async-start(), calls=%async_computation.9 | async-start | bytes 2359296 | tf_op jit(solution)/shard_map/all_gather | solution.py:105
  9.4 385.5 %all-gather.16.cloned.1.call-start = ((), (), s32[]{:S(2)}) async-start(), calls=%async_computation.11 | async-start | bytes 2359296 | tf_op jit(solution)/shard_map/all_gather | solution.py:111
  10.0 544.2 %all-reduce.9.cloned.1.call-start = ((), (), s32[]{:S(2)}) async-start(), calls=%async_computation.12 | async-start | bytes 16777216 | tf_op jit(solution)/shard_map/psum | solution.py:146
  10.1 58.8 %copy-start.1 = (bf16[1024,2048]{1,0:T(8,128)(2,1)S(1)}, bf16[1024,2048]{1,0:T(8,128)(2,1)}, u32[]{:S(2)}) copy-start(bf16[1024,2048]{1,0:T(8,128)(2,1)} %param.18) | copy-start | bytes 12582916
  13.4 55.5 %copy-start.16 = (f32[1024]{0:T(1024)}, f32[1024]{0:T(1024)S(1)}, u32[]{:S(2)}) copy-start(f32[1024]{0:T(1024)S(1)} %fusion.140) | copy-start | bytes 12292
  36.4 32.5 %copy-start.14 = (f32[8,1,256]{2,1,0:T(1,128)}, f32[8,1,256]{2,1,0:T(1,128)S(1)}, u32[]{:S(2)}) copy-start(f32[8,1,256]{2,1,0:T(1,128)S(1)} %convert_element_type.131) | copy-start | bytes 24580
  391.4 11.2 copy-start.5
  402.6 246.1 %all-gather.18.cloned.1.call-start = ((), (), s32[]{:S(2)}) async-start(), calls=%async_computation.13 | async-start | bytes 6488064 | tf_op jit(solution)/shard_map/all_gather | solution.py:107
  403.2 338.2 %all-gather.20.cloned.1.call-start = ((), (), s32[]{:S(2)}) async-start(), calls=%async_computation.14 | async-start | bytes 6488064 | tf_op jit(solution)/shard_map/all_gather | solution.py:108
  404.0 430.8 %all-gather.22.cloned.1.call-start = ((), (), s32[]{:S(2)}) async-start(), calls=%async_computation.15 | async-start | bytes 6488064 | tf_op jit(solution)/shard_map/all_gather | solution.py:112
  404.7 616.8 %all-reduce.11.cloned.1.call-start = ((), (), s32[]{:S(2)}) async-start(), calls=%async_computation.16 | async-start | bytes 16777216 | tf_op jit(solution)/shard_map/psum | solution.py:180
  850.4 10.9 copy-start.30
  850.4 10.9 copy-start.29
  850.4 10.9 copy-start.22
  870.3 781.4 %all-reduce.13.cloned.1.call-start = ((), (), s32[]{:S(2)}) async-start(), calls=%async_computation.25 | async-start | bytes 16777216 | tf_op jit(solution)/shard_map/psum | solution.py:155
  1021.5 8.2 copy-start.4
  1021.5 9.4 copy-start.6
  1041.4 431.7 %copy-start.10 = (f32[1024,64]{0,1:T(8,128)S(1)}, f32[1024,64]{0,1:T(8,128)}, u32[]{:S(2)}) copy-start(f32[1024,64]{0,1:T(8,128)} %get-tuple-element.870) | copy-start | bytes 786436
  1498.5 225.8 %reduce-scatter.17.cloned.1.call-start = ((), (), s32[]{:S(2)}) async-start(), calls=%async_computation.21 | async-start | bytes 2359296 | tf_op jit(solution)/shard_map/reduce_scatter | solution.py:218
  1506.8 331.1 %reduce-scatter.23.cloned.1.call-start = ((), (), s32[]{:S(2)}) async-start(), calls=%async_computation.24 | async-start | bytes 6488064 | tf_op jit(solution)/shard_map/reduce_scatter | solution.py:221
  1517.7 386.5 %reduce-scatter.15.cloned.1.call-start = ((), (), s32[]{:S(2)}) async-start(), calls=%async_computation.20 | async-start | bytes 589824 | tf_op jit(solution)/shard_map/reduce_scatter | solution.py:213
  1521.8 473.9 %reduce-scatter.11.cloned.1.call-start = ((), (), s32[]{:S(2)}) async-start(), calls=%async_computation.18 | async-start | bytes 4718592 | tf_op jit(solution)/shard_map/reduce_scatter | solution.py:211
  1528.3 559.4 %reduce-scatter.13.cloned.1.call-start = ((), (), s32[]{:S(2)}) async-start(), calls=%async_computation.19 | async-start | bytes 4718592 | tf_op jit(solution)/shard_map/reduce_scatter | solution.py:212
  1536.1 643.7 %reduce-scatter.9.cloned.1.call-start = ((), (), s32[]{:S(2)}) async-start(), calls=%async_computation.17 | async-start | bytes 4718592 | tf_op jit(solution)/shard_map/reduce_scatter | solution.py:210
  1542.7 833.6 %reduce-scatter.19.cloned.1.call-start = ((), (), s32[]{:S(2)}) async-start(), calls=%async_computation.22 | async-start | bytes 12976128 | tf_op jit(solution)/shard_map/reduce_scatter | solution.py:214
  1554.9 1017.4 %reduce-scatter.21.cloned.1.call-start = ((), (), s32[]{:S(2)}) async-start(), calls=%async_computation.23 | async-start | bytes 12976128 | tf_op jit(solution)/shard_map/reduce_scatter | solution.py:215
  1567.0 84.7 %copy-start.15 = (f32[8,1,256]{2,1,0:T(1,128)S(1)}, f32[8,1,256]{2,1,0:T(1,128)}, u32[]{:S(2)}) copy-start(f32[8,1,256]{2,1,0:T(1,128)} %copy-done.14) | copy-start | bytes 24580
  1567.0 84.7 %copy-start.17 = (f32[1024]{0:T(1024)S(1)}, f32[1024]{0:T(1024)}, u32[]{:S(2)}) copy-start(f32[1024]{0:T(1024)} %copy-done.16) | copy-start | bytes 12292
  1651.6 74.4 %copy-start.19 = (f32[1024]{0:T(1024)S(1)}, f32[1024]{0:T(1024)}, u32[]{:S(2)}) copy-start(f32[1024]{0:T(1024)} %copy-done.18) | copy-start | bytes 12292
  (17 other events, 55.5 us)
Sparse Core Ops, SparseCore 0:
  10.1 54.1 all-gather.13
  66.4 48.7 all-gather.9
  117.4 47.6 all-gather.11
  166.9 48.9 all-gather.15
  402.8 151.3 all-reduce.8
  556.2 92.4 all-gather.17
  650.9 90.4 all-gather.19
  743.5 91.3 all-gather.21
  870.4 151.0 all-reduce.10
  1498.6 152.9 all-reduce.12
  1655.2 69.0 reduce-scatter.16
  1727.8 109.9 reduce-scatter.22
  1841.8 62.4 reduce-scatter.14
  1908.3 87.3 reduce-scatter.10
  1999.7 87.9 reduce-scatter.12
  2091.8 87.9 reduce-scatter.8
  2183.8 192.4 reduce-scatter.18
  2380.3 191.9 reduce-scatter.20
where the time goes:
time: 2590 us; the launch traced here: 2580 us
  waiting for transfers between devices  1530 us (59%)
  matrix products  649 us (25%)
  other arithmetic  155 us (6%)
  local copies, waits for them, and re-layouts  111 us (4%)
  blocking collectives  111 us (4%)
    reduce_scatter x1, waiting for transfers between devices, per_device(): lax.psum_scatter(grad_gate, 'dp', scatter_dimension=0, tiled=True)  197 us
    reduce_scatter x1, waiting for transfers between devices, per_device(): lax.psum_scatter(grad_up, 'dp', scatter_dimension=0, tiled=True)  196 us
    dot_general x24, matrix products, matmul_low(): return jnp.dot(left, right, preferred_element_type=jnp.float32)  191 us
    dot_general x48, matrix products, span_step(): mixing = jnp.einsum('tj,tsj->ts', slot_probs, weighted, precision=highest)  166 us
    psum x1, waiting for transfers between devices, per_device(): lax.psum(matmul_low(d_gate_low, full_gate.T) + matmul_low(d_up_low, full_...  137 us
    psum x1, waiting for transfers between devices, per_device(): resid = rows_in + lax.psum(matmul_low(mixed_low, full_out), 'head')  131 us
    dot_general x32, matrix products, span_step(): jnp.einsum('tsj,ts->tj', weighted, inner_products, precision=highest)  106 us
    reduce_scatter x1, waiting for transfers between devices, per_device(): lax.psum_scatter(grad_down.astype(jnp.bfloat16), 'dp', scatter_dimension=...  94.6 us
  transfers between devices with their start and end apart: 18, of which 16 were waited for; matrix products, arithmetic and copies ran while one was open for 15% of the time, Pallas kernels for 0%

commit v1 on v0

v1 whole, which is shorter than its diff:
```python
import jax
import jax.numpy as jnp
from jax import lax
from jax.experimental import pallas as pl
from jax.experimental.pallas import tpu as pltpu
from jax.sharding import PartitionSpec as P

BLOCK = 64
TILE = 128
epsilon = 1e-06


def split_low(values):
    high = values.astype(jnp.bfloat16)
    return high, (values - high.astype(jnp.float32)).astype(jnp.bfloat16)


def dot_nn(left, right):
    return lax.dot_general(left, right, (((1,), (0,)), ((), ())), preferred_element_type=jnp.float32)


def dot_nt(left, right):
    return lax.dot_general(left, right, (((1,), (1,)), ((), ())), preferred_element_type=jnp.float32)


def lane_place():
    lanes = lax.broadcasted_iota(jnp.int32, (BLOCK, TILE), 1)
    return lanes, jnp.bitwise_and(lanes, BLOCK - 1)


def prefix_sum(values, place):
    step = 1
    while step < BLOCK:
        values = values + jnp.where(place >= step, pltpu.roll(values, step, 1), 0.0)
        step *= 2
    return values


def suffix_sum(values, place):
    step = 1
    while step < BLOCK:
        values = values + jnp.where(place < BLOCK - step, pltpu.roll(values, TILE - step, 1), 0.0)
        step *= 2
    return values


def skew(square, forward):
    rows = lax.broadcasted_iota(jnp.int32, (TILE, TILE), 0)
    step = 1
    while step < TILE:
        moved = pltpu.roll(square, step if forward else TILE - step, 1)
        square = jnp.where(jnp.bitwise_and(rows, step) != 0, moved, square)
        step *= 2
    return square


def to_band(square):
    return skew(square, False).T


def from_band(band):
    return skew(band.T, True)


def gate_terms(logits, valid, place):
    log_sig = jnp.minimum(logits, 0.0) - jnp.log1p(jnp.exp(-jnp.abs(logits)))
    logdecay = valid * log_sig * 0.125
    decay = jnp.exp(logdecay)
    series = -logdecay * (1.0 + logdecay * (0.5 + logdecay * (1.0 / 6.0 + logdecay * (1.0 / 24.0))))
    writes = valid * jnp.where(logdecay > -0.03, series, 1.0 - decay)
    inside = jnp.where(place == 0, 0.0, decay)
    before = prefix_sum(logdecay, place)
    after = suffix_sum(logdecay, place) - logdecay
    return decay, writes, inside, before, after


def stacked(values, lanes):
    return jnp.concatenate(
        [jnp.where(lanes < BLOCK, values, 0.0), jnp.where(lanes < BLOCK, 0.0, values)], axis=0
    )


def own_block(square, lanes):
    return jnp.where(lanes < BLOCK, square[:BLOCK], square[BLOCK:])


def forward_kernel(
    length_ref, qkv_ref, logit_ref, bias_ref,
    mixed_ref, state_ref, prob_ref, score_ref, mix_ref,
    gate_ref, carry_ref, band_ref,
):
    width = mixed_ref.shape[1]
    tiles = mixed_ref.shape[0] // TILE
    scale = width ** -0.5
    lanes, place = lane_place()
    bias = bias_ref[...]

    def valid_of(tile):
        return (lanes + tile * TILE < length_ref[0]).astype(jnp.float32)

    def rows_of(tile):
        return pl.ds(pl.multiple_of(tile * TILE, TILE), TILE)

    def gather_writes(tile, none):
        logits = logit_ref[tile] + bias
        decay, writes, inside, before, after = gate_terms(logits, valid_of(tile), place)
        gate_ref[tile, 0] = writes
        gate_ref[tile, 1] = inside
        gate_ref[tile, 2] = jnp.exp(before)
        gate_ref[tile, 3] = jnp.exp(before + after)
        high, low = split_low(stacked(jnp.exp(after) * writes, lanes))
        rows = qkv_ref[rows_of(tile), width:]
        added = dot_nn(high, rows) + dot_nn(low, rows)
        state_ref[tile] = added
        return none

    lax.fori_loop(0, tiles, gather_writes, 0)

    carry_ref[...] = jnp.zeros_like(carry_ref)

    def run_states(tile, none):
        for part in range(2):
            span = pl.ds(part * BLOCK, BLOCK)
            fade = gate_ref[tile, 3, :, part * BLOCK : part * BLOCK + 1]
            carried = carry_ref[...]
            added = state_ref[tile, span, :]
            state_ref[tile, span, :] = carried
            carry_ref[...] = fade * carried + added
        return none

    lax.fori_loop(0, tiles, run_states, 0)

    def mix_tile(tile, none):
        queries = qkv_ref[rows_of(tile), :width]
        key_rows = qkv_ref[rows_of(tile), width : 2 * width]
        value_rows = qkv_ref[rows_of(tile), 2 * width :]
        writes, inside, fade = gate_ref[tile, 0], gate_ref[tile, 1], gate_ref[tile, 2]
        band_ref[...] = to_band(dot_nt(queries, key_rows) * scale)
        high, low = split_low(state_ref[tile, :, :width])
        carried = own_block(dot_nt(high, queries) + dot_nt(low, queries), lanes)

        def lag_score(lag, carry):
            weighted, total = carry
            total = total + weighted * band_ref[pl.ds(jnp.bitwise_and(TILE - lag, TILE - 1), 1), :]
            return inside * pltpu.roll(weighted, 1, 1), total

        _, scores = lax.fori_loop(
            0, BLOCK, lag_score, (writes, fade * carried * scale), unroll=8
        )
        top = jnp.max(scores, axis=0, keepdims=True)
        raised = jnp.exp(scores - top)
        probs = raised / jnp.sum(raised, axis=0, keepdims=True)
        score_ref[tile] = scores
        prob_ref[tile] = probs
        band_ref[...] = jnp.zeros_like(band_ref)

        def lag_mix(lag, weighted):
            band_ref[pl.ds(jnp.bitwise_and(TILE - lag, TILE - 1), 1), :] = jnp.sum(
                probs * weighted, axis=0, keepdims=True
            )
            return inside * pltpu.roll(weighted, 1, 1)

        lax.fori_loop(0, BLOCK, lag_mix, writes, unroll=8)
        mixing = from_band(band_ref[...]).astype(jnp.bfloat16)
        mix_ref[tile] = mixing
        reach = stacked(probs * fade, lanes).T.astype(jnp.bfloat16)
        result = dot_nn(mixing, value_rows) + dot_nn(reach, state_ref[tile, :, width:].astype(jnp.bfloat16))
        rows = lax.broadcasted_iota(jnp.int32, (TILE, 1), 0) + tile * TILE
        mixed_ref[rows_of(tile), :] = jnp.where(rows < length_ref[0], result, 0.0).astype(jnp.bfloat16)
        return none

    lax.fori_loop(0, tiles, mix_tile, 0)


def backward_kernel(
    length_ref, qkv_ref, logit_ref, bias_ref, back_ref, state_ref, prob_ref, score_ref, mix_ref,
    d_qkv_ref, d_logit_ref, d_bias_ref,
    adjoint_ref, slope_ref, gain_ref, key_band_ref, value_band_ref, band_ref, carry_ref, end_ref, cross_ref,
):
    width = back_ref.shape[1]
    tiles = back_ref.shape[0] // TILE
    scale = width ** -0.5
    lanes, place = lane_place()
    bias = bias_ref[...]

    def valid_of(tile):
        return (lanes + tile * TILE < length_ref[0]).astype(jnp.float32)

    def rows_of(tile):
        return pl.ds(pl.multiple_of(tile * TILE, TILE), TILE)

    def back_of(tile):
        rows = lax.broadcasted_iota(jnp.int32, (TILE, 1), 0) + tile * TILE
        return jnp.where(rows < length_ref[0], back_ref[rows_of(tile), :], jnp.zeros((), back_ref.dtype))

    def slopes(tile, none):
        logits = logit_ref[tile] + bias
        decay, writes, inside, before, after = gate_terms(logits, valid_of(tile), place)
        fade = jnp.exp(before)
        queries = qkv_ref[rows_of(tile), :width]
        key_rows = qkv_ref[rows_of(tile), width : 2 * width]
        value_rows = qkv_ref[rows_of(tile), 2 * width :]
        back = back_of(tile)
        probs = prob_ref[tile]
        key_band_ref[...] = to_band(dot_nt(queries, key_rows) * scale)
        value_band_ref[...] = to_band(dot_nt(back, value_rows))
        high, low = split_low(state_ref[tile, :, width:])
        carried = own_block(dot_nt(high, back) + dot_nt(low, back), lanes)

        def lag_gain(lag, carry):
            weighted, total = carry
            total = total + weighted * value_band_ref[pl.ds(jnp.bitwise_and(TILE - lag, TILE - 1), 1), :]
            return inside * pltpu.roll(weighted, 1, 1), total

        _, gains = lax.fori_loop(0, BLOCK, lag_gain, (writes, fade * carried), unroll=8)
        d_scores = probs * (gains - jnp.sum(probs * gains, axis=0, keepdims=True))
        slope_ref[tile] = d_scores
        band_ref[...] = jnp.zeros_like(band_ref)

        def lag_mix(lag, weighted):
            band_ref[pl.ds(jnp.bitwise_and(TILE - lag, TILE - 1), 1), :] = jnp.sum(
                d_scores * weighted, axis=0, keepdims=True
            )
            return inside * pltpu.roll(weighted, 1, 1)

        lax.fori_loop(0, BLOCK, lag_mix, writes, unroll=8)
        mixing = (from_band(band_ref[...]) * scale).astype(jnp.bfloat16)

        def lag_write(count, total):
            lag = BLOCK - 1 - count
            row = pl.ds(jnp.bitwise_and(TILE - lag, TILE - 1), 1)
            return (
                d_scores * key_band_ref[row, :]
                + probs * value_band_ref[row, :]
                + pltpu.roll(inside * total, TILE - 1, 1)
            )

        gain_ref[tile, 0] = lax.fori_loop(0, BLOCK, lag_write, jnp.zeros((BLOCK, TILE), jnp.float32), unroll=8)
        gain_ref[tile, 1] = d_scores * score_ref[tile] + probs * gains
        gain_ref[tile, 2] = decay
        gain_ref[tile, 3] = writes
        gain_ref[tile, 4] = jnp.exp(after)
        gain_ref[tile, 5] = jnp.exp(before + after)
        reach = stacked(d_scores * fade * scale, lanes)
        reach_low = reach.astype(jnp.bfloat16)
        d_qkv_ref[rows_of(tile), :width] = (
            dot_nn(mixing, key_rows)
            + dot_nn(reach.T.astype(jnp.bfloat16), state_ref[tile, :, :width].astype(jnp.bfloat16))
        ).astype(jnp.bfloat16)
        adjoint_ref[tile, :, :width] = dot_nn(reach_low, queries)
        adjoint_ref[tile, :, width:] = dot_nn(stacked(probs * fade, lanes).astype(jnp.bfloat16), back)
        d_qkv_ref[rows_of(tile), width : 2 * width] = dot_nn(mixing.T, queries).astype(jnp.bfloat16)
        d_qkv_ref[rows_of(tile), 2 * width :] = dot_nn(mix_ref[tile].T, back).astype(jnp.bfloat16)
        return none

    lax.fori_loop(0, tiles, slopes, 0)

    carry_ref[...] = jnp.zeros_like(carry_ref)
    end_ref[...] = jnp.zeros_like(end_ref)

    def run_adjoints(count, none):
        tile = tiles - 1 - count
        for part in (1, 0):
            span = pl.ds(part * BLOCK, BLOCK)
            fade = gain_ref[tile, 5, :, part * BLOCK : part * BLOCK + 1]
            carried = carry_ref[...]
            added = adjoint_ref[tile, span, :]
            adjoint_ref[tile, span, :] = carried
            cross_ref[tile, span, :] = jnp.broadcast_to(
                jnp.sum(carried * end_ref[...], axis=1, keepdims=True), (BLOCK, TILE)
            )
            end_ref[...] = state_ref[tile, span, :]
            carry_ref[...] = fade * carried + added
        return none

    lax.fori_loop(0, tiles, run_adjoints, 0)

    d_bias_ref[...] = jnp.zeros_like(d_bias_ref)

    def finish(tile, none):
        key_rows = qkv_ref[rows_of(tile), width : 2 * width]
        value_rows = qkv_ref[rows_of(tile), 2 * width :]
        adjoint = adjoint_ref[tile]
        high, low = split_low(adjoint)
        rows = qkv_ref[rows_of(tile), width:]
        carried = own_block(dot_nt(high, rows) + dot_nt(low, rows), lanes)
        decay, writes, rest = gain_ref[tile, 2], gain_ref[tile, 3], gain_ref[tile, 4]
        d_writes = gain_ref[tile, 0] + rest * carried
        tail = stacked(rest * writes, lanes).T.astype(jnp.bfloat16)
        d_qkv_ref[rows_of(tile), width:] = (
            d_qkv_ref[rows_of(tile), width:].astype(jnp.float32) + dot_nn(tail, high)
        ).astype(jnp.bfloat16)
        cross = own_block(cross_ref[tile], lanes)
        d_decay = suffix_sum(gain_ref[tile, 1] - writes * d_writes, place) + cross - decay * d_writes
        logits = logit_ref[tile] + bias
        d_logit = valid_of(tile) * d_decay * jax.nn.sigmoid(-logits) * 0.125
        d_bias_ref[...] += jnp.broadcast_to(jnp.sum(d_logit, axis=1, keepdims=True), (BLOCK, TILE))
        d_logit_ref[tile] = d_logit.astype(jnp.bfloat16)
        return none

    lax.fori_loop(0, tiles, finish, 0)


def mixer_forward(length, qkv, logits, bias):
    rows, width = qkv.shape[0], qkv.shape[1] // 3
    tiles = rows // TILE
    f32 = jnp.float32
    return pl.pallas_call(
        forward_kernel,
        out_shape=(
            jax.ShapeDtypeStruct((rows, width), jnp.bfloat16),
            jax.ShapeDtypeStruct((tiles, TILE, 2 * width), f32),
            jax.ShapeDtypeStruct((tiles, BLOCK, TILE), f32),
            jax.ShapeDtypeStruct((tiles, BLOCK, TILE), f32),
            jax.ShapeDtypeStruct((tiles, TILE, TILE), jnp.bfloat16),
        ),
        in_specs=[pl.BlockSpec(memory_space=pltpu.SMEM)] + [pl.BlockSpec(memory_space=pltpu.VMEM)] * 3,
        out_specs=[pl.BlockSpec(memory_space=pltpu.VMEM)] * 5,
        scratch_shapes=[
            pltpu.VMEM((tiles, 4, BLOCK, TILE), f32),
            pltpu.VMEM((BLOCK, 2 * width), f32),
            pltpu.VMEM((TILE, TILE), f32),
        ],
        name="mixer_forward",
    )(length, qkv, logits, bias)


def mixer_backward(length, qkv, logits, bias, back, saved):
    rows, width = qkv.shape[0], qkv.shape[1] // 3
    tiles = rows // TILE
    f32 = jnp.float32
    return pl.pallas_call(
        backward_kernel,
        out_shape=(
            jax.ShapeDtypeStruct((rows, 3 * width), jnp.bfloat16),
            jax.ShapeDtypeStruct((tiles, BLOCK, TILE), jnp.bfloat16),
            jax.ShapeDtypeStruct((BLOCK, TILE), f32),
        ),
        in_specs=[pl.BlockSpec(memory_space=pltpu.SMEM)] + [pl.BlockSpec(memory_space=pltpu.VMEM)] * 8,
        out_specs=[pl.BlockSpec(memory_space=pltpu.VMEM)] * 3,
        scratch_shapes=[
            pltpu.VMEM((tiles, TILE, 2 * width), f32),
            pltpu.VMEM((tiles, BLOCK, TILE), f32),
            pltpu.VMEM((tiles, 6, BLOCK, TILE), f32),
            pltpu.VMEM((TILE, TILE), f32),
            pltpu.VMEM((TILE, TILE), f32),
            pltpu.VMEM((TILE, TILE), f32),
            pltpu.VMEM((BLOCK, 2 * width), f32),
            pltpu.VMEM((BLOCK, 2 * width), f32),
            pltpu.VMEM((tiles, TILE, TILE), f32),
        ],
        name="mixer_backward",
    )(length, qkv, logits, bias, back, *saved)


def to_low(values):
    return values.astype(jnp.bfloat16)


def to_wide(values):
    return values.astype(jnp.float32)


def dot_tn(left, right):
    return lax.dot_general(left, right, (((0,), (0,)), ((), ())), preferred_element_type=jnp.float32)


def after(values, *earlier):
    return lax.optimization_barrier((values,) + earlier)[0]


def ring_order(size):
    return list(range(0, size, 2)) + list(range(size - 1 - size % 2, 0, -2))


def hop_pairs(order, hop):
    size = len(order)
    return [(order[i], order[(i + hop) % size]) for i in range(size)]


def ring_gather(shard, order):
    size = len(order)
    up, down = hop_pairs(order, 1), hop_pairs(order, -1)
    pieces = [shard] + [None] * (size - 1)
    from_low, from_high = shard, shard
    for step in range(1, (size + 1) // 2):
        from_low = lax.ppermute(from_low, "dp", up)
        from_high = lax.ppermute(from_high, "dp", down)
        pieces[size - step], pieces[step] = from_low, from_high
    if size % 2 == 0:
        half = shard.shape[0] // 2
        first = lax.ppermute(from_low[:half], "dp", up)
        second = lax.ppermute(from_high[half:], "dp", down)
        pieces[size // 2] = jnp.concatenate([first, second], axis=0)
    return pieces


def ring_scatter(piece_of, order):
    size = len(order)
    up, down = hop_pairs(order, 1), hop_pairs(order, -1)
    half_count = (size - 1) // 2
    up_sum, down_sum = None, None
    if size % 2 == 0:
        farthest = piece_of(size // 2)
        half = farthest.shape[0] // 2
        up_half = lax.ppermute(to_low(farthest[:half]), "dp", up)
        down_half = lax.ppermute(to_low(farthest[half:]), "dp", down)
        up_sum = jnp.concatenate([to_wide(up_half), jnp.zeros(up_half.shape, jnp.float32)], axis=0)
        down_sum = jnp.concatenate([jnp.zeros(down_half.shape, jnp.float32), to_wide(down_half)], axis=0)
    for step in range(half_count, 0, -1):
        up_piece, down_piece = to_wide(piece_of(step)), to_wide(piece_of(size - step))
        if up_sum is not None:
            up_piece, down_piece = up_piece + up_sum, down_piece + down_sum
        up_sum = to_wide(lax.ppermute(to_low(up_piece), "dp", up))
        down_sum = to_wide(lax.ppermute(to_low(down_piece), "dp", down))
    total = to_wide(piece_of(0))
    if up_sum is not None:
        total = total + up_sum + down_sum
    return total


def spread_rows(rows, order):
    size = len(order)
    parts = [rows] + [lax.ppermute(rows, "dp", hop_pairs(order, -hop)) for hop in range(1, size)]
    return jnp.stack(parts)


def scatter_rows(rows, order):
    size = len(order)
    total = rows[0]
    for hop in range(1, size):
        total = total + lax.ppermute(rows[hop], "dp", hop_pairs(order, hop))
    return total


def move_kernel(places_ref, source_ref, target_ref):
    target_ref[...] = source_ref[...]


def move_columns(matrix, places, inverse):
    size = places.shape[0]
    rows, columns = matrix.shape
    width = columns // size
    if width % 128:
        split = matrix.reshape(rows, size, width)
        if inverse:
            places = jnp.argsort(places)
        return jnp.take(split, places, axis=1).reshape(rows, columns)

    def plain(step, places_ref):
        return (0, step)

    def placed(step, places_ref):
        return (0, places_ref[step])

    return pl.pallas_call(
        move_kernel,
        out_shape=jax.ShapeDtypeStruct(matrix.shape, matrix.dtype),
        grid_spec=pltpu.PrefetchScalarGridSpec(
            num_scalar_prefetch=1,
            grid=(size,),
            in_specs=[pl.BlockSpec((rows, width), plain if inverse else placed)],
            out_specs=pl.BlockSpec((rows, width), placed if inverse else plain),
        ),
        cost_estimate=pl.CostEstimate(flops=0, bytes_accessed=2 * matrix.size * matrix.dtype.itemsize, transcendentals=0),
        name="move_columns",
    )(places, matrix)


def head_sum(values, parts=2):
    heads = lax.axis_size("head")
    near = [(i, i ^ 1) for i in range(heads)]
    far = [(i, i ^ 2) for i in range(heads)]
    even = jnp.bitwise_and(lax.axis_index("head"), 1) == 0
    rows = values.shape[0] // parts
    sums = []
    for part in range(parts):
        piece = values[part * rows : (part + 1) * rows]
        low_half, high_half = piece[: rows // 2], piece[rows // 2 :]
        sent = to_low(jnp.where(even, high_half, low_half))
        kept = to_wide(jnp.where(even, low_half, high_half))
        kept = to_low(kept + to_wide(lax.ppermute(sent, "head", near)))
        kept = to_low(to_wide(kept) + to_wide(lax.ppermute(kept, "head", far)))
        other = lax.ppermute(kept, "head", near)
        sums += [jnp.where(even, kept, other), jnp.where(even, other, kept)]
    return jnp.concatenate(sums, axis=0)


def per_device(
    inputs,
    lengths,
    gain_attn,
    w_query,
    w_key,
    w_value,
    w_slot,
    gate_bias,
    w_out,
    gain_ffn,
    w_gate,
    w_up,
    w_down,
    cotangent,
):
    size = lax.axis_size("dp")
    order = ring_order(size)
    place = [order.index(i) for i in range(size)]
    me = lax.axis_index("dp")
    spot = jnp.array(place, jnp.int32)[me]
    places = jnp.array(order + order, jnp.int32)[spot + jnp.arange(size, dtype=jnp.int32)]
    share = gain_attn.shape[0]
    width = w_query.shape[1]
    hidden_count = w_gate.shape[1]
    cut = (hidden_count // 128 + 1) // 2 * 128
    spans = [(0, cut), (cut, hidden_count)]

    gains = spread_rows(jnp.concatenate([gain_attn, gain_ffn]), order)
    gain_one = to_wide(gains[:, :share].reshape(1, size * share))
    gain_two = to_wide(gains[:, share:].reshape(1, size * share))

    out_rows = w_out.T
    down_rows = w_down.T
    mix_shard = jnp.concatenate([w_query, w_key, w_value, w_slot], axis=1)
    mix_pieces = ring_gather(mix_shard, order)
    out_pieces = ring_gather(after(out_rows, mix_pieces[2]), order)
    feed_pieces = []
    earlier = mix_pieces[size // 2]
    for low, high in spans:
        shard = jnp.concatenate([w_gate[:, low:high], w_up[:, low:high], down_rows[:, low:high]], axis=1)
        pieces = ring_gather(after(shard, earlier), order)
        earlier = pieces[size // 2 - 1]
        feed_pieces.append(pieces)

    def joined(pieces, low, high):
        return jnp.concatenate([piece[:, low:high] for piece in pieces], axis=0)

    rows_in = to_wide(move_columns(inputs, places, False))
    back_low = move_columns(cotangent, places, False)
    factor_one = lax.rsqrt(jnp.mean(rows_in * rows_in, axis=-1, keepdims=True) + epsilon)
    normed = to_low(rows_in * factor_one * gain_one)

    full_qkv = joined(mix_pieces, 0, 3 * width)
    full_slot = joined(mix_pieces, 3 * width, mix_shard.shape[1])
    qkv = to_low(dot_nn(normed, full_qkv))
    logits = lax.dot_general(full_slot, normed, (((0,), (1,)), ((), ())), preferred_element_type=jnp.float32)
    slots, length = logits.shape
    logits = logits.reshape(slots, length // TILE, TILE).transpose(1, 0, 2)
    bias = gate_bias[:, None]
    mixed, *saved = mixer_forward(lengths, qkv, logits, bias)
    full_out = jnp.concatenate(out_pieces, axis=0)
    resid = rows_in + to_wide(head_sum(dot_nt(mixed, full_out)))
    factor_two = lax.rsqrt(jnp.mean(resid * resid, axis=-1, keepdims=True) + epsilon)
    normed_two = to_low(resid * factor_two * gain_two)

    result, d_normed_two, feed_grads = None, None, []
    for pieces, (low, high) in zip(feed_pieces, spans):
        count = high - low
        full_gate = joined(pieces, 0, count)
        full_up = joined(pieces, count, 2 * count)
        full_down = joined(pieces, 2 * count, 3 * count)
        gate_act = dot_nn(normed_two, full_gate)
        up_act = dot_nn(normed_two, full_up)
        d_hidden = dot_nn(back_low, full_down)
        sigma = jax.nn.sigmoid(gate_act)
        gated = gate_act * sigma
        hidden = to_low(gated * up_act)
        d_up = to_low(d_hidden * gated)
        d_gate = to_low(d_hidden * up_act * (sigma * (1.0 + gate_act * (1.0 - sigma))))
        grads = [
            to_low(dot_tn(normed_two, d_gate)),
            to_low(dot_tn(normed_two, d_up)),
            to_low(dot_tn(back_low, hidden)),
        ]

        def piece_of(index, grads=grads):
            return jnp.concatenate([grad[index * share : (index + 1) * share] for grad in grads], axis=1)

        feed_grads.append(ring_scatter(piece_of, order))
        term = dot_nt(hidden, full_down)
        result = term if result is None else result + term
        term = dot_nt(d_gate, full_gate) + dot_nt(d_up, full_up)
        d_normed_two = term if d_normed_two is None else d_normed_two + term

    d_normed_two = to_wide(head_sum(d_normed_two))
    hat_two = resid * factor_two
    grad_gain_two = jnp.sum(d_normed_two * hat_two, axis=0)
    scaled = gain_two * d_normed_two
    d_resid = to_wide(back_low) + factor_two * (
        scaled - hat_two * jnp.mean(scaled * hat_two, axis=-1, keepdims=True)
    )
    d_attn = to_low(d_resid)
    d_mixed = to_low(dot_nn(d_attn, full_out))
    grad_out = to_low(dot_tn(d_attn, mixed))
    d_qkv, d_logits, d_bias = mixer_backward(lengths, qkv, logits, bias, d_mixed, saved)
    d_logits = d_logits.transpose(1, 0, 2).reshape(slots, length)
    d_normed = head_sum(
        dot_nt(d_qkv, full_qkv)
        + lax.dot_general(d_logits, full_slot, (((0,), (1,)), ((), ())), preferred_element_type=jnp.float32)
    )
    grad_qkv = to_low(dot_tn(normed, d_qkv))
    grad_slot = to_low(lax.dot_general(normed, d_logits, (((0,), (1,)), ((), ())), preferred_element_type=jnp.float32))

    def out_piece(index):
        return grad_out[index * share : (index + 1) * share]

    def mix_piece(index):
        rows = slice(index * share, (index + 1) * share)
        return jnp.concatenate([grad_qkv[rows], grad_slot[rows]], axis=1)

    out_grad = ring_scatter(out_piece, order)
    mix_grad = ring_scatter(mix_piece, order)

    output = move_columns(to_low(resid + to_wide(head_sum(after(result, d_mixed)))), places, True)
    d_normed = to_wide(d_normed)
    hat_one = rows_in * factor_one
    grad_gain_one = jnp.sum(d_normed * hat_one, axis=0)
    scaled = gain_one * d_normed
    grad_inputs = move_columns(
        d_resid + factor_one * (scaled - hat_one * jnp.mean(scaled * hat_one, axis=-1, keepdims=True)),
        places,
        True,
    )
    small = jnp.concatenate(
        [
            grad_gain_one.reshape(size, share),
            grad_gain_two.reshape(size, share),
            jnp.broadcast_to(d_bias[:, 0], (size, slots)),
        ],
        axis=1,
    )
    small = scatter_rows(small, order)

    def feed_columns(index):
        columns = []
        for grad, (low, high) in zip(feed_grads, spans):
            count = high - low
            columns.append(grad[:, index * count : (index + 1) * count])
        return jnp.concatenate(columns, axis=1)

    return (
        output,
        grad_inputs,
        small[:share],
        mix_grad[:, :width],
        mix_grad[:, width : 2 * width],
        mix_grad[:, 2 * width : 3 * width],
        mix_grad[:, 3 * width :],
        small[2 * share :],
        out_grad.T,
        small[share : 2 * share],
        feed_columns(0),
        feed_columns(1),
        feed_columns(2).T,
    )


def solution(mesh):
    in_specs = (
        P("dp", None),
        P("dp"),
        P("dp"),
        P("dp", "head"),
        P("dp", "head"),
        P("dp", "head"),
        P("dp", "head"),
        P("head"),
        P("head", "dp"),
        P("dp"),
        P("dp", "head"),
        P("dp", "head"),
        P("head", "dp"),
        P("dp", None),
    )
    out_specs = (
        P("dp", None),
        P("dp", None),
        P("dp"),
        P("dp", "head"),
        P("dp", "head"),
        P("dp", "head"),
        P("dp", "head"),
        P("head"),
        P("head", "dp"),
        P("dp"),
        P("dp", "head"),
        P("dp", "head"),
        P("head", "dp"),
    )
    return jax.shard_map(
        per_device, mesh=mesh, in_specs=in_specs, out_specs=out_specs, check_vma=False
    )
```

time: 2590 us -> 1110 us (0.43)
  waiting for transfers between devices: 1530 us -> 363 us
  matrix products: 649 us -> 147 us
  Pallas kernels: 0 us -> 263 us
  blocking collectives: 111 us -> 0 us
  starting transfers between devices: 0.72 us -> 99.9 us
  local copies, waits for them, and re-layouts: 111 us -> 84.2 us
    reduce_scatter x8 -> x0, waiting for transfers between devices: 854 us -> none  [the longest x1 197 us: per_device(): lax.psum_scatter(grad_gate, 'dp', scatter_dimension=0, tiled=True)]
    dot_general x424 -> x27, matrix products: 649 us -> 147 us  [the longest x8 58.7 us: dot_nt(): lax.dot_general(left, right, (((1,), (1,)), ((), ())), preferred_element_...]
    ppermute x0 -> x102, waiting for transfers between devices: none -> 363 us  [the longest x8 88.8 us: head_sum(): kept = to_low(to_wide(kept) + to_wide(lax.ppermute(kept, 'head', far)))]
    psum x3 -> x0, waiting for transfers between devices: 351 us -> none  [the longest x1 137 us: per_device(): lax.psum(matmul_low(d_gate_low, full_gate.T) + matmul_low(d_up_low, full_...]
    all_gather x7 -> x0, waiting for transfers between devices: 323 us -> none  [the longest x1 82.7 us: per_device(): lax.all_gather(w_gate, 'dp', axis=0, tiled=True)]
    pallas_call x0 -> x6, Pallas kernels: none -> 263 us  [the longest x1 136 us: mixer_backward(): pl.pallas_call(backward_kernel, out_shape=(jax.ShapeDtypeStruct((rows, 3...]
    ppermute x0 -> x102, starting transfers between devices: none -> 99.9 us  [the longest x12 14.2 us: ring_scatter(): down_sum = to_wide(lax.ppermute(to_low(down_piece), 'dp', down))]
    squeeze x112 -> x0, local copies, waits for them, and re-layouts: 72.4 us -> none  [the longest x80 72.3 us: slot_mixer(): lax.scan(jax.checkpoint(span_step), start_state, (blocked(queries), block...]
  transfers between devices with their start and end apart: 18 -> 102, of which waited for: 16 -> 39; matrix products, arithmetic and copies ran while one was open for 15% -> 30% of each run, Pallas kernels for 0% -> 15%
where the time goes in v1:
time: 1110 us
  waiting for transfers between devices  363 us (33%)
  Pallas kernels  263 us (24%)
  matrix products  147 us (13%)
  other arithmetic  146 us (13%)
  starting transfers between devices  99.9 us (9%)
  local copies, waits for them, and re-layouts  84.2 us (8%)
    pallas_call x1, Pallas kernels, mixer_backward(): pl.pallas_call(backward_kernel, out_shape=(jax.ShapeDtypeStruct((rows, 3...  136 us
    pallas_call x1, Pallas kernels, mixer_forward(): pl.pallas_call(forward_kernel, out_shape=(jax.ShapeDtypeStruct((rows, wid...  95.6 us
    ppermute x8, waiting for transfers between devices, head_sum(): kept = to_low(to_wide(kept) + to_wide(lax.ppermute(kept, 'head', far)))  88.8 us
    ppermute x12, waiting for transfers between devices, ring_gather(): from_low = lax.ppermute(from_low, 'dp', up)  81.6 us
    convert_element_type x40, other arithmetic, to_low(): return values.astype(jnp.bfloat16)  70.9 us
    ppermute x12, waiting for transfers between devices, ring_scatter(): up_sum = to_wide(lax.ppermute(to_low(up_piece), 'dp', up))  62.3 us
    dot_general x8, matrix products, dot_nt(): lax.dot_general(left, right, (((1,), (1,)), ((), ())), preferred_element_...  58.7 us
    unnamed x296, local copies, waits for them, and re-layouts  54.5 us
  transfers between devices with their start and end apart: 102, of which 39 were waited for; matrix products, arithmetic and copies ran while one was open for 30% of the time, Pallas kernels for 15%

profile of v1, /device:TPU:0, one launch (start us, length us, event | category | flops | bytes accessed | tf_op | source)
XLA Modules:
  0.0 1107.5 jit_solution(13429121874207118654)
XLA Ops:
  42.4 9.2 collective-permute-done.6
  56.8 16.0 %collective-permute-done.11 = bf16[256,1600]{0,1:T(8,128)(2,1)S(1)} collective-permute-done((bf16[256,1600]{0,1:T(8,128)(2,1)S(1)}, bf16[256,1600]{0,1:T(8,128)(2,1)S(1)}, u32[]{:S(2)}, u32[]{:S(2)}) %collective-permute-start.11) | collective-permute-done | bytes 819232 | tf_op jit(solution)/shard_map/ppermute | solution.py:387
  83.5 15.4 %collective-permute-done.19 = bf16[256,512]{0,1:T(8,128)(2,1)S(1)} collective-permute-done((bf16[256,512]{0,1:T(8,128)(2,1)S(1)}, bf16[256,512]{0,1:T(8,128)(2,1)S(1)}, u32[]{:S(2)}, u32[]{:S(2)}) %collective-permute-start.19) | collective-permute-done | bytes 262176 | tf_op jit(solution)/shard_map/ppermute | solution.py:387
  124.7 10.3 convolution_convert_fusion.1.qkv_ref
  137.2 95.6 %mixer_forward.1 = (bf16[1024,512]{1,0:T(8,128)(2,1)}, f32[8,128,1024]{2,1,0:T(8,128)}, f32[8,64,128]{2,1,0:T(8,128)}, f32[8,64,128]{2,1,0:T(8,128)}, bf16[8,128,128]{2,1,0:T(8,128)(2,1)}) custom-call(s32[1]{0:T(128)S(6)} %copy.154.length_ref, bf16[1024,1536]{1,0:T(8,128)(2,1)} %convolution_convert_fusion.1.qkv_ref, f32[8,64,128]{2,1,0:T(8,128)} %bitcast.87, ...), custom_call_target="tpu_custom_call" | custom-call | tf_op jit(solution)/shard_map/mixer_forward/pallas_call | solution.py:308
  279.1 19.9 %collective-permute-done.27 = bf16[256,2048]{1,0:T(8,128)(2,1)} collective-permute-done((bf16[256,2048]{1,0:T(8,128)(2,1)S(1)}, bf16[256,2048]{1,0:T(8,128)(2,1)}, u32[]{:S(2)}, u32[]{:S(2)}) %collective-permute-start.27) | collective-permute-done | bytes 1048608 | tf_op jit(solution)/shard_map/ppermute | solution.py:483
  311.6 20.0 %collective-permute-done.34 = bf16[256,2304]{0,1:T(8,128)(2,1)S(1)} collective-permute-done((bf16[256,2304]{0,1:T(8,128)(2,1)S(1)}, bf16[256,2304]{0,1:T(8,128)(2,1)S(1)}, u32[]{:S(2)}, u32[]{:S(2)}) %collective-permute-start.34) | collective-permute-done | bytes 1179680 | tf_op jit(solution)/shard_map/ppermute | solution.py:387
  333.4 7.9 multiply_convert_fusion
  348.0 28.7 %collective-permute-done.36 = bf16[128,2304]{0,1:T(8,128)(2,1)S(1)} collective-permute-done((bf16[128,2304]{0,1:T(8,128)(2,1)S(1)}, bf16[128,2304]{0,1:T(8,128)(2,1)S(1)}, u32[]{:S(2)}, u32[]{:S(2)}) %collective-permute-start.36) | collective-permute-done | bytes 589856 | tf_op jit(solution)/shard_map/ppermute | solution.py:393
  382.2 8.2 fusion.54
  436.0 7.7 fusion.57
  445.6 11.1 collective-permute-done.38
  459.0 22.4 %collective-permute-done.87 = bf16[256,2304]{0,1:T(8,128)(2,1)S(1)} collective-permute-done((bf16[256,2304]{0,1:T(8,128)(2,1)S(1)}, bf16[256,2304]{0,1:T(8,128)(2,1)S(1)}, u32[]{:S(2)}, u32[]{:S(2)}) %collective-permute-start.87) | collective-permute-done | bytes 1179680 | tf_op jit(solution)/shard_map/ppermute | solution.py:414
  483.4 19.1 %collective-permute-done.42 = bf16[256,1920]{0,1:T(8,128)(2,1)S(1)} collective-permute-done((bf16[256,1920]{0,1:T(8,128)(2,1)S(1)}, bf16[256,1920]{0,1:T(8,128)(2,1)S(1)}, u32[]{:S(2)}, u32[]{:S(2)}) %collective-permute-start.42) | collective-permute-done | bytes 983072 | tf_op jit(solution)/shard_map/ppermute | solution.py:387
  506.8 28.7 %collective-permute-done.43 = bf16[128,1920]{0,1:T(8,128)(2,1)S(1)} collective-permute-done((bf16[128,1920]{0,1:T(8,128)(2,1)S(1)}, bf16[128,1920]{0,1:T(8,128)(2,1)S(1)}, u32[]{:S(2)}, u32[]{:S(2)}) %collective-permute-start.43) | collective-permute-done | bytes 491552 | tf_op jit(solution)/shard_map/ppermute | solution.py:392
  572.6 10.5 add_add_fusion
  596.5 8.0 convolution_add_fusion.1
  613.2 8.4 collective-permute-done.89
  626.1 16.2 %collective-permute-done.95 = bf16[256,1920]{0,1:T(8,128)(2,1)} collective-permute-done((bf16[256,1920]{0,1:T(8,128)(2,1)S(1)}, bf16[256,1920]{0,1:T(8,128)(2,1)}, u32[]{:S(2)}, u32[]{:S(2)}) %collective-permute-start.95) | collective-permute-done | bytes 983072 | tf_op jit(solution)/shard_map/ppermute | solution.py:414
  646.7 11.8 %collective-permute-done.49 = bf16[256,2048]{1,0:T(8,128)(2,1)S(1)} collective-permute-done((bf16[256,2048]{1,0:T(8,128)(2,1)S(1)}, bf16[256,2048]{1,0:T(8,128)(2,1)S(1)}, u32[]{:S(2)}, u32[]{:S(2)}) %collective-permute-start.49) | collective-permute-done | bytes 1048608 | tf_op jit(solution)/shard_map/ppermute | solution.py:483
  659.0 8.0 collective-permute-done.96
  675.1 8.6 fusion.12
  683.7 13.8 %fusion.11 = f32[1024,2048]{1,0:T(8,128)S(1)} fusion(bf16[1024,2048]{1,0:T(8,128)(2,1)S(1)} %copy-done.19, bf16[1024,2048]{1,0:T(8,128)(2,1)S(1)} %copy-done.3, f32[1024]{0:T(1024)S(1)} %broadcast_multiply_fusion.1, f32[2048]{0:T(1024)S(1)} %bitcast.96, f32[1024]{0:T(1024)S(1)} %copy-done.84, bf16[256,2048]{1,0:T(8,128)(2,1)S(1)} %get-tuple-element.173, ...), kind=kLoop, calls=%fused_computation.18 | loop fusion | flops 52428800 | bytes 25182208 | tf_op jit(solution)/shard_map/add | solution.py:588
  705.0 136.2 %mixer_backward.1 = (bf16[1024,1536]{1,0:T(8,128)(2,1)}, bf16[8,64,128]{2,1,0:T(8,128)(2,1)}, f32[64,128]{1,0:T(8,128)}) custom-call(s32[1]{0:T(128)S(6)} %copy.154.length_ref, bf16[1024,1536]{1,0:T(8,128)(2,1)} %convolution_convert_fusion.1.qkv_ref, f32[8,64,128]{2,1,0:T(8,128)} %bitcast.88, f32[64,1]{1,0:T(8,128)} %copy.54.bias_ref, ...), custom_call_target="tpu_custom_call" | custom-call | tf_op jit(solution)/shard_map/mixer_backward/pallas_call | solution.py:332
  850.5 8.5 convolution_convert_fusion
  864.1 10.2 convolution_add_fusion
  926.8 14.9 %collective-permute-done.84 = bf16[256,512]{1,0:T(8,128)(2,1)S(1)} collective-permute-done((bf16[256,512]{1,0:T(8,128)(2,1)S(1)}, bf16[256,512]{1,0:T(8,128)(2,1)S(1)}, u32[]{:S(2)}, u32[]{:S(2)}) %collective-permute-start.84) | collective-permute-done | bytes 262176 | tf_op jit(solution)/shard_map/ppermute | solution.py:415
  975.4 17.5 %collective-permute-done.61 = bf16[256,2048]{1,0:T(8,128)(2,1)} collective-permute-done((bf16[256,2048]{1,0:T(8,128)(2,1)}, bf16[256,2048]{1,0:T(8,128)(2,1)}, u32[]{:S(2)}, u32[]{:S(2)}) %collective-permute-start.61) | collective-permute-done | bytes 1048608 | tf_op jit(solution)/shard_map/ppermute | solution.py:483
  995.7 19.6 %collective-permute-done.52 = bf16[256,2048]{1,0:T(8,128)(2,1)} collective-permute-done((bf16[256,2048]{1,0:T(8,128)(2,1)}, bf16[256,2048]{1,0:T(8,128)(2,1)}, u32[]{:S(2)}, u32[]{:S(2)}) %collective-permute-start.52) | collective-permute-done | bytes 1048608 | tf_op jit(solution)/shard_map/ppermute | solution.py:483
  1018.2 15.2 %collective-permute-done.55 = bf16[256,2048]{1,0:T(8,128)(2,1)S(1)} collective-permute-done((bf16[256,2048]{1,0:T(8,128)(2,1)}, bf16[256,2048]{1,0:T(8,128)(2,1)S(1)}, u32[]{:S(2)}, u32[]{:S(2)}) %collective-permute-start.55) | collective-permute-done | bytes 1048608 | tf_op jit(solution)/shard_map/ppermute | solution.py:483
  1068.5 20.8 %fusion.8 = (f32[1024,2048]{1,0:T(8,128)}, bf16[1024,2048]{1,0:T(8,128)(2,1)}) fusion(f32[1024,2048]{1,0:T(8,128)} %copy-done.16, bf16[1024,2048]{1,0:T(8,128)(2,1)S(1)} %copy-done.6, f32[1024]{0:T(1024)S(1)} %broadcast_multiply_fusion, f32[2048]{0:T(1024)S(1)} %bitcast.102, f32[1024]{0:T(1024)S(1)} %copy-done.96, bf16[256,2048]{1,0:T(8,128)(2,1)} %copy-done.26, ...), kind=kLoop, calls=%fused_computation.15 | loop fusion | flops 71303168 | bytes 37765120 | tf_op jit(solution)/shard_map/add | solution.py:619
  1089.2 9.6 move_columns.7
  (639 shorter events, 446.1 us)
Async XLA Ops:
  8.7 43.0 %collective-permute-start.10 = (bf16[256,1600]{0,1:T(8,128)(2,1)}, bf16[256,1600]{0,1:T(8,128)(2,1)S(1)}, u32[]{:S(2)}, u32[]{:S(2)}) collective-permute-start(bf16[256,1600]{0,1:T(8,128)(2,1)} %pad_maximum_fusion.9), channel_id=1, source_target_pairs={{0,8},{8,16},{16,24},{24,28},{28,20},{20,12},{12,4},{4,0},{1,9},{9... | collective-permute-start | bytes 2457608 | tf_op jit(solution)/shard_map/ppermute | solution.py:387
  55.5 54.7 %collective-permute-start.9 = (bf16[256,1600]{0,1:T(8,128)(2,1)S(1)}, bf16[256,1600]{0,1:T(8,128)(2,1)S(1)}, u32[]{:S(2)}, u32[]{:S(2)}) collective-permute-start(bf16[256,1600]{0,1:T(8,128)(2,1)S(1)} %collective-permute-done.8), channel_id=1, source_target_pairs={{0,4},{8,0},{16,8},{24,16},{28,24},{20,28},{12,20},{4,12},{1,5},{9... | collective-permute-start | bytes 2457608 | tf_op jit(solution)/shard_map/ppermute | solution.py:388
  72.8 39.5 %collective-permute-start.12 = (bf16[256,1600]{0,1:T(8,128)(2,1)S(1)}, bf16[256,1600]{0,1:T(8,128)(2,1)S(1)}, u32[]{:S(2)}, u32[]{:S(2)}) collective-permute-start(bf16[256,1600]{0,1:T(8,128)(2,1)S(1)} %collective-permute-done.11), channel_id=1, source_target_pairs={{0,8},{8,16},{16,24},{24,28},{28,20},{20,12},{12,4},{4,0},{1,9},{9... | collective-permute-start | bytes 2457608 | tf_op jit(solution)/shard_map/ppermute | solution.py:387
  252.8 46.3 %collective-permute-start.27 = (bf16[256,2048]{1,0:T(8,128)(2,1)S(1)}, bf16[256,2048]{1,0:T(8,128)(2,1)}, u32[]{:S(2)}, u32[]{:S(2)}) collective-permute-start(bf16[256,2048]{1,0:T(8,128)(2,1)S(1)} %get-tuple-element.88), channel_id=1, source_target_pairs={{0,2},{1,3},{2,0},{3,1},{4,6},{5,7},{6,4},{7,5},{8,10},{9,11},{10,... | collective-permute-start | bytes 3145736 | tf_op jit(solution)/shard_map/ppermute | solution.py:483
  303.0 38.4 %collective-permute-start.31 = (bf16[256,2304]{0,1:T(8,128)(2,1)S(1)}, bf16[256,2304]{0,1:T(8,128)(2,1)S(1)}, u32[]{:S(2)}, u32[]{:S(2)}) collective-permute-start(bf16[256,2304]{0,1:T(8,128)(2,1)S(1)} %collective-permute-done.30), channel_id=1, source_target_pairs={{0,4},{8,0},{16,8},{24,16},{28,24},{20,28},{12,20},{4,12},{1,5},{9... | collective-permute-start | bytes 3538952 | tf_op jit(solution)/shard_map/ppermute | solution.py:388
  341.3 87.1 %collective-permute-start.37 = (bf16[256,1920]{0,1:T(8,128)(2,1)S(1)}, bf16[256,1920]{0,1:T(8,128)(2,1)S(1)}, u32[]{:S(2)}, u32[]{:S(2)}) collective-permute-start(bf16[256,1920]{0,1:T(8,128)(2,1)S(1)} %pad_maximum_fusion.7), channel_id=1, source_target_pairs={{0,4},{8,0},{16,8},{24,16},{28,24},{20,28},{12,20},{4,12},{1,5},{9... | collective-permute-start | bytes 2949128 | tf_op jit(solution)/shard_map/ppermute | solution.py:388
  341.7 87.4 %collective-permute-start.40 = (bf16[256,1920]{0,1:T(8,128)(2,1)S(1)}, bf16[256,1920]{0,1:T(8,128)(2,1)S(1)}, u32[]{:S(2)}, u32[]{:S(2)}) collective-permute-start(bf16[256,1920]{0,1:T(8,128)(2,1)S(1)} %pad_maximum_fusion.7), channel_id=1, source_target_pairs={{0,8},{8,16},{16,24},{24,28},{28,20},{20,12},{12,4},{4,0},{1,9},{9... | collective-permute-start | bytes 2949128 | tf_op jit(solution)/shard_map/ppermute | solution.py:387
  435.3 46.1 %collective-permute-start.87 = (bf16[256,2304]{0,1:T(8,128)(2,1)S(1)}, bf16[256,2304]{0,1:T(8,128)(2,1)S(1)}, u32[]{:S(2)}, u32[]{:S(2)}) collective-permute-start(bf16[256,2304]{0,1:T(8,128)(2,1)S(1)} %add_convert_fusion.6), channel_id=1, source_target_pairs={{0,8},{8,16},{16,24},{24,28},{28,20},{20,12},{12,4},{4,0},{1,9},{9... | collective-permute-start | bytes 3538952 | tf_op jit(solution)/shard_map/ppermute | solution.py:414
  444.0 59.2 %collective-permute-start.91 = (bf16[256,2304]{0,1:T(8,128)(2,1)S(1)}, bf16[256,2304]{0,1:T(8,128)(2,1)S(1)}, u32[]{:S(2)}, u32[]{:S(2)}) collective-permute-start(bf16[256,2304]{0,1:T(8,128)(2,1)S(1)} %add_convert_fusion.3), channel_id=1, source_target_pairs={{0,4},{8,0},{16,8},{24,16},{28,24},{20,28},{12,20},{4,12},{1,5},{9... | collective-permute-start | bytes 3538952 | tf_op jit(solution)/shard_map/ppermute | solution.py:415
  456.7 49.3 %collective-permute-start.39 = (bf16[256,1920]{0,1:T(8,128)(2,1)S(1)}, bf16[256,1920]{0,1:T(8,128)(2,1)S(1)}, u32[]{:S(2)}, u32[]{:S(2)}) collective-permute-start(bf16[256,1920]{0,1:T(8,128)(2,1)S(1)} %collective-permute-done.38), channel_id=1, source_target_pairs={{0,4},{8,0},{16,8},{24,16},{28,24},{20,28},{12,20},{4,12},{1,5},{9... | collective-permute-start | bytes 2949128 | tf_op jit(solution)/shard_map/ppermute | solution.py:388
  458.2 44.3 %collective-permute-start.42 = (bf16[256,1920]{0,1:T(8,128)(2,1)S(1)}, bf16[256,1920]{0,1:T(8,128)(2,1)S(1)}, u32[]{:S(2)}, u32[]{:S(2)}) collective-permute-start(bf16[256,1920]{0,1:T(8,128)(2,1)S(1)} %collective-permute-done.41), channel_id=1, source_target_pairs={{0,8},{8,16},{16,24},{24,28},{28,20},{20,12},{12,4},{4,0},{1,9},{9... | collective-permute-start | bytes 2949128 | tf_op jit(solution)/shard_map/ppermute | solution.py:387
  482.8 108.1 %collective-permute-start.88 = (bf16[256,2304]{0,1:T(8,128)(2,1)}, bf16[256,2304]{0,1:T(8,128)(2,1)}, u32[]{:S(2)}, u32[]{:S(2)}) collective-permute-start(bf16[256,2304]{0,1:T(8,128)(2,1)} %add_convert_fusion.5), channel_id=1, source_target_pairs={{0,8},{8,16},{16,24},{24,28},{28,20},{20,12},{12,4},{4,0},{1,9},{9... | collective-permute-start | bytes 3538952 | tf_op jit(solution)/shard_map/ppermute | solution.py:414
  504.5 88.2 %collective-permute-start.92 = (bf16[256,2304]{0,1:T(8,128)(2,1)}, bf16[256,2304]{0,1:T(8,128)(2,1)}, u32[]{:S(2)}, u32[]{:S(2)}) collective-permute-start(bf16[256,2304]{0,1:T(8,128)(2,1)} %add_convert_fusion.2), channel_id=1, source_target_pairs={{0,4},{8,0},{16,8},{24,16},{28,24},{20,28},{12,20},{4,12},{1,5},{9... | collective-permute-start | bytes 3538952 | tf_op jit(solution)/shard_map/ppermute | solution.py:415
  668.3 212.8 %collective-permute-start.97 = (bf16[256,1920]{0,1:T(8,128)(2,1)}, bf16[256,1920]{0,1:T(8,128)(2,1)}, u32[]{:S(2)}, u32[]{:S(2)}) collective-permute-start(bf16[256,1920]{0,1:T(8,128)(2,1)} %add_convert_fusion.26), channel_id=1, source_target_pairs={{0,8},{8,16},{16,24},{24,28},{28,20},{20,12},{12,4},{4,0},{1,9},{9... | collective-permute-start | bytes 2949128 | tf_op jit(solution)/shard_map/ppermute | solution.py:414
  670.1 211.5 %collective-permute-start.101 = (bf16[256,1920]{0,1:T(8,128)(2,1)}, bf16[256,1920]{0,1:T(8,128)(2,1)}, u32[]{:S(2)}, u32[]{:S(2)}) collective-permute-start(bf16[256,1920]{0,1:T(8,128)(2,1)} %add_convert_fusion.23), channel_id=1, source_target_pairs={{0,4},{8,0},{16,8},{24,16},{28,24},{20,28},{12,20},{4,12},{1,5},{9... | collective-permute-start | bytes 2949128 | tf_op jit(solution)/shard_map/ppermute | solution.py:415
  849.1 50.6 %collective-permute-start.82 = (bf16[128,512]{1,0:T(8,128)(2,1)}, bf16[128,512]{1,0:T(8,128)(2,1)}, u32[]{:S(2)}, u32[]{:S(2)}) collective-permute-start(bf16[128,512]{1,0:T(8,128)(2,1)} %get-tuple-element.161), channel_id=1, source_target_pairs={{0,4},{8,0},{16,8},{24,16},{28,24},{20,28},{12,20},{4,12},{1,5},{9... | collective-permute-start | bytes 393224 | tf_op jit(solution)/shard_map/ppermute | solution.py:407
  863.5 38.6 %collective-permute-start.70 = (bf16[128,1600]{0,1:T(8,128)(2,1)}, bf16[128,1600]{0,1:T(8,128)(2,1)}, u32[]{:S(2)}, u32[]{:S(2)}) collective-permute-start(bf16[128,1600]{0,1:T(8,128)(2,1)} %get-tuple-element.236), channel_id=1, source_target_pairs={{0,8},{8,16},{16,24},{24,28},{28,20},{20,12},{12,4},{4,0},{1,9},{9... | collective-permute-start | bytes 1228808 | tf_op jit(solution)/shard_map/ppermute | solution.py:406
  880.1 38.0 %collective-permute-start.57 = (bf16[256,2048]{1,0:T(8,128)(2,1)}, bf16[256,2048]{1,0:T(8,128)(2,1)}, u32[]{:S(2)}, u32[]{:S(2)}) collective-permute-start(bf16[256,2048]{1,0:T(8,128)(2,1)} %get-tuple-element.77), channel_id=1, source_target_pairs={{0,1},{1,0},{2,3},{3,2},{4,5},{5,4},{6,7},{7,6},{8,9},{9,8},{10,11... | collective-permute-start | bytes 3145736 | tf_op jit(solution)/shard_map/ppermute | solution.py:482
  881.1 38.0 %collective-permute-start.60 = (bf16[256,2048]{1,0:T(8,128)(2,1)}, bf16[256,2048]{1,0:T(8,128)(2,1)}, u32[]{:S(2)}, u32[]{:S(2)}) collective-permute-start(bf16[256,2048]{1,0:T(8,128)(2,1)} %get-tuple-element.78), channel_id=1, source_target_pairs={{0,1},{1,0},{2,3},{3,2},{4,5},{5,4},{6,7},{7,6},{8,9},{9,8},{10,11... | collective-permute-start | bytes 3145736 | tf_op jit(solution)/shard_map/ppermute | solution.py:482
  900.8 47.8 %collective-permute-start.51 = (bf16[256,2048]{1,0:T(8,128)(2,1)}, bf16[256,2048]{1,0:T(8,128)(2,1)S(1)}, u32[]{:S(2)}, u32[]{:S(2)}) collective-permute-start(bf16[256,2048]{1,0:T(8,128)(2,1)} %get-tuple-element.81), channel_id=1, source_target_pairs={{0,1},{1,0},{2,3},{3,2},{4,5},{5,4},{6,7},{7,6},{8,9},{9,8},{10,11... | collective-permute-start | bytes 3145736 | tf_op jit(solution)/shard_map/ppermute | solution.py:482
  912.1 37.8 %collective-permute-start.54 = (bf16[256,2048]{1,0:T(8,128)(2,1)S(1)}, bf16[256,2048]{1,0:T(8,128)(2,1)S(1)}, u32[]{:S(2)}, u32[]{:S(2)}) collective-permute-start(bf16[256,2048]{1,0:T(8,128)(2,1)S(1)} %copy-done.63), channel_id=1, source_target_pairs={{0,1},{1,0},{2,3},{3,2},{4,5},{5,4},{6,7},{7,6},{8,9},{9,8},{10,11... | collective-permute-start | bytes 3145736 | tf_op jit(solution)/shard_map/ppermute | solution.py:482
  953.2 39.6 %collective-permute-start.61 = (bf16[256,2048]{1,0:T(8,128)(2,1)}, bf16[256,2048]{1,0:T(8,128)(2,1)}, u32[]{:S(2)}, u32[]{:S(2)}) collective-permute-start(bf16[256,2048]{1,0:T(8,128)(2,1)} %get-tuple-element.76), channel_id=1, source_target_pairs={{0,2},{1,3},{2,0},{3,1},{4,6},{5,7},{6,4},{7,5},{8,10},{9,11},{10,... | collective-permute-start | bytes 3145736 | tf_op jit(solution)/shard_map/ppermute | solution.py:483
  955.9 59.4 %collective-permute-start.52 = (bf16[256,2048]{1,0:T(8,128)(2,1)}, bf16[256,2048]{1,0:T(8,128)(2,1)}, u32[]{:S(2)}, u32[]{:S(2)}) collective-permute-start(bf16[256,2048]{1,0:T(8,128)(2,1)} %get-tuple-element.79), channel_id=1, source_target_pairs={{0,2},{1,3},{2,0},{3,1},{4,6},{5,7},{6,4},{7,5},{8,10},{9,11},{10,... | collective-permute-start | bytes 3145736 | tf_op jit(solution)/shard_map/ppermute | solution.py:483
  965.7 67.7 %collective-permute-start.55 = (bf16[256,2048]{1,0:T(8,128)(2,1)}, bf16[256,2048]{1,0:T(8,128)(2,1)S(1)}, u32[]{:S(2)}, u32[]{:S(2)}) collective-permute-start(bf16[256,2048]{1,0:T(8,128)(2,1)} %get-tuple-element.80), channel_id=1, source_target_pairs={{0,2},{1,3},{2,0},{3,1},{4,6},{5,7},{6,4},{7,5},{8,10},{9,11},{10,... | collective-permute-start | bytes 3145736 | tf_op jit(solution)/shard_map/ppermute | solution.py:483
  969.0 65.8 %collective-permute-start.73 = (bf16[256,1600]{0,1:T(8,128)(2,1)S(1)}, bf16[256,1600]{0,1:T(8,128)(2,1)S(1)}, u32[]{:S(2)}, u32[]{:S(2)}) collective-permute-start(bf16[256,1600]{0,1:T(8,128)(2,1)S(1)} %add_convert_fusion.32), channel_id=1, source_target_pairs={{0,8},{8,16},{16,24},{24,28},{28,20},{20,12},{12,4},{4,0},{1,9},{9... | collective-permute-start | bytes 2457608 | tf_op jit(solution)/shard_map/ppermute | solution.py:414
  971.5 63.7 %collective-permute-start.77 = (bf16[256,1600]{0,1:T(8,128)(2,1)S(1)}, bf16[256,1600]{0,1:T(8,128)(2,1)S(1)}, u32[]{:S(2)}, u32[]{:S(2)}) collective-permute-start(bf16[256,1600]{0,1:T(8,128)(2,1)S(1)} %add_convert_fusion.29), channel_id=1, source_target_pairs={{0,4},{8,0},{16,8},{24,16},{28,24},{20,28},{12,20},{4,12},{1,5},{9... | collective-permute-start | bytes 2457608 | tf_op jit(solution)/shard_map/ppermute | solution.py:415
  992.8 50.6 %collective-permute-start.59 = (bf16[256,2048]{1,0:T(8,128)(2,1)}, bf16[256,2048]{1,0:T(8,128)(2,1)}, u32[]{:S(2)}, u32[]{:S(2)}) collective-permute-start(bf16[256,2048]{1,0:T(8,128)(2,1)} %add_convert_fusion.9), channel_id=1, source_target_pairs={{0,1},{1,0},{2,3},{3,2},{4,5},{5,4},{6,7},{7,6},{8,9},{9,8},{10,11... | collective-permute-start | bytes 3145736 | tf_op jit(solution)/shard_map/ppermute | solution.py:484
  1057.2 48.9 %collective-permute-start.65 = (f32[576]{0:T(1024)S(1)}, f32[576]{0:T(1024)S(1)}, u32[]{:S(2)}, u32[]{:S(2)}) collective-permute-start(f32[576]{0:T(1024)S(1)} %get-tuple-element.72), channel_id=1, source_target_pairs={{0,24},{8,28},{16,20},{24,12},{28,4},{20,0},{12,8},{4,16},{1,25},{... | collective-permute-start | bytes 6920 | tf_op jit(solution)/shard_map/ppermute | solution.py:432
  1058.7 47.5 %collective-permute-start.66 = (f32[576]{0:T(1024)S(1)}, f32[576]{0:T(1024)S(1)}, u32[]{:S(2)}, u32[]{:S(2)}) collective-permute-start(f32[576]{0:T(1024)S(1)} %get-tuple-element.71), channel_id=1, source_target_pairs={{0,28},{8,20},{16,12},{24,4},{28,0},{20,8},{12,16},{4,24},{1,29},{... | collective-permute-start | bytes 6920 | tf_op jit(solution)/shard_map/ppermute | solution.py:432
  1063.2 43.0 %collective-permute-start.67 = (f32[576]{0:T(1024)S(1)}, f32[576]{0:T(1024)S(1)}, u32[]{:S(2)}, u32[]{:S(2)}) collective-permute-start(f32[576]{0:T(1024)S(1)} %get-tuple-element.70), channel_id=1, source_target_pairs={{0,20},{8,12},{16,4},{24,0},{28,8},{20,16},{12,24},{4,28},{1,21},{... | collective-permute-start | bytes 6920 | tf_op jit(solution)/shard_map/ppermute | solution.py:432
  1066.1 40.1 %collective-permute-start.68 = (f32[576]{0:T(1024)S(1)}, f32[576]{0:T(1024)S(1)}, u32[]{:S(2)}, u32[]{:S(2)}) collective-permute-start(f32[576]{0:T(1024)S(1)} %get-tuple-element.69), channel_id=1, source_target_pairs={{0,12},{8,4},{16,0},{24,8},{28,16},{20,24},{12,28},{4,20},{1,13},{... | collective-permute-start | bytes 6920 | tf_op jit(solution)/shard_map/ppermute | solution.py:432
  1068.2 38.0 %collective-permute-start.69 = (f32[576]{0:T(1024)S(1)}, f32[576]{0:T(1024)S(1)}, u32[]{:S(2)}, u32[]{:S(2)}) collective-permute-start(f32[576]{0:T(1024)S(1)} %get-tuple-element.68), channel_id=1, source_target_pairs={{0,4},{8,0},{16,8},{24,16},{28,24},{20,28},{12,20},{4,12},{1,5},{9... | collective-permute-start | bytes 6920 | tf_op jit(solution)/shard_map/ppermute | solution.py:432
  (193 other events, 3395.9 us)
